TPU v7x, 32 devices: a whole 2x2x4 slice. The times are simulated.
32 devices in a mesh: dp: 4 (over y, x), expert: 8 (over z, core).
Axes of the slice: x: 2, y: 2, z: 4, core: 2. Of those that a mesh axis runs over, the one named last changes fastest.
Arguments:
- tokens: bfloat16 [8192, 2048], P(('dp', 'expert')), may hold values from -6 to 6
- expert_ids: int32 [8192, 8], P(('dp', 'expert')), may hold values from 0 to 15, all different within a row; in each aligned block of 256 rows (0 to 255, 256 to 511, ...) at most 160 rows name the same one
- route_probs: float32 [8192, 8], P(('dp', 'expert')), may hold values from 0.05 to 1
- w_gate_up: bfloat16 [16, 2048, 1536], P('expert', 'dp'), may hold values from -0.125 to 0.125
- w_down: bfloat16 [16, 768, 2048], P('expert', None, 'dp'), may hold values from -0.21875 to 0.21875
Outputs:
- moe_out: bfloat16 [8192, 2048], P(('dp', 'expert'))
Inputs may be any that keep to these rules, and one draw needn't show every extreme that they name: `expert_ids`: each row names 8 different experts. Among the rows of one device no expert is named more than 160 times, and in every draw some expert is named exactly 160 times in some device's rows.
All inputs are finite; a program needn't handle non-finite values.
Results may differ from a plain program's by a relative error of at most 0.0057.
Values may be sent and summed in bfloat16 or wider, within the bound.
A program may use at most 128 MiB of HBM per device.

v0:
```python
import jax
import jax.numpy as jnp
from jax import lax
from jax.sharding import PartitionSpec as P


def shards(tokens, expert_ids, route_probs, w_gate_up, w_down):
    owners = lax.axis_size("expert")
    local_count = w_gate_up.shape[0]
    experts = owners * local_count
    tok_rows = tokens.shape[0]
    model_width = tokens.shape[1]
    top_count = expert_ids.shape[1]
    capacity = 5 * tok_rows * top_count // (4 * experts)
    hidden_units = w_down.shape[1]
    flat_ids = expert_ids.reshape(-1)
    onehot = (flat_ids[:, None] == jnp.arange(experts, dtype=jnp.int32)[None, :]).astype(jnp.int32)
    before = jnp.cumsum(onehot, axis=0) - onehot
    slot_of = jnp.sum(before * onehot, axis=1)
    target = flat_ids * capacity + slot_of
    copies = jnp.repeat(tokens, top_count, axis=0)
    send_buffer = jnp.zeros((experts * capacity, model_width), jnp.bfloat16).at[target].set(copies)
    send_buffer = send_buffer.reshape(experts, capacity, model_width)
    received = lax.all_to_all(send_buffer, "expert", split_axis=0, concat_axis=1, tiled=True)
    returned_list = []
    for local_expert in range(local_count):
        rows_in = received[local_expert]
        joined = jnp.dot(
            rows_in,
            lax.all_gather(w_gate_up[local_expert], "dp", axis=0, tiled=True),
            preferred_element_type=jnp.float32,
        )
        hidden = (jax.nn.silu(joined[:, :hidden_units]) * joined[:, hidden_units:]).astype(
            jnp.bfloat16
        )
        returned_list.append(
            lax.all_to_all(
                jnp.dot(
                    hidden,
                    lax.all_gather(w_down[local_expert], "dp", axis=1, tiled=True),
                    preferred_element_type=jnp.float32,
                ).astype(jnp.bfloat16),
                "expert",
                split_axis=0,
                concat_axis=0,
                tiled=True,
            )
        )
    returned = jnp.concatenate(returned_list, axis=0)
    source_rows = (
        flat_ids % local_count * (owners * capacity) + flat_ids // local_count * capacity + slot_of
    )
    gathered = returned[source_rows].reshape(tok_rows, top_count, model_width)
    weights = route_probs / jnp.sum(route_probs, axis=1, keepdims=True)
    combined = jnp.sum(gathered.astype(jnp.float32) * weights[:, :, None], axis=1)
    return combined.astype(jnp.bfloat16)


def solution(mesh):
    return jax.shard_map(
        shards,
        mesh=mesh,
        in_specs=(
            P(("dp", "expert"), None),
            P(("dp", "expert"), None),
            P(("dp", "expert"), None),
            P("expert", "dp", None),
            P("expert", None, "dp"),
        ),
        out_specs=P(("dp", "expert"), None),
        check_vma=False,
    )
```

profile of v0, /device:TPU:0, one launch (start us, length us, event | category | flops | bytes accessed | tf_op | source)
XLA Modules:
  0.0 597.6 jit_solution(10399717120854872721)
XLA Ops:
  6.5 0.0 copy-start
  6.5 0.9 copy.7
  7.5 0.1 eq.31
  7.6 0.1 eq.27
  7.7 0.1 reshape.185
  7.8 4.5 reduce-window.6
  12.4 0.4 slice_reduce_fusion
  12.8 0.2 reduce-window.9
  13.0 0.1 broadcast_add_fusion
  13.1 0.1 fusion.19
  13.2 0.1 compare_select_fusion
  13.2 0.0 copy-done
  13.3 17.9 %scatter_custom_fusion = bf16[2560,2048]{1,0:T(8,128)(2,1)} fusion(s32[2048]{0:T(1024)S(1)} %bitcast.60, bf16[]{:T(256)} %constant.36.clone.1, bf16[256,2048]{1,0:T(8,128)(2,1)S(1)} %copy-done), kind=kCustom, calls=%fused_computation.5 | custom fusion | bytes 11534338 | tf_op jit(solution)/shard_map/scatter | solution.py:22
  31.1 6.4 %all-to-all-start = ((bf16[16,160,2048]{2,1,0:T(8,128)(2,1)}), bf16[16,160,2048]{2,1,0:T(8,128)(2,1)}, u32[]{:S(2)}, u32[]{:S(2)}) async-start(bf16[16,160,2048]{2,1,0:T(8,128)(2,1)} %bitcast.51), calls=%async_computation | async-start | bytes 20971520 | tf_op jit(solution)/shard_map/all_to_all | solution.py:24
  37.5 0.0 copy-start.2
  37.5 0.0 all-gather.9.cloned.1.call-start
  37.5 3.8 fusion.27
  41.4 0.0 all-gather.9.cloned.1.call-update
  41.4 0.0 all-gather.11.cloned.1.call-start
  41.5 0.0 copy-done.2
  41.5 1.3 fusion.28
  42.8 0.0 all-gather.11.cloned.1.call-update
  42.8 0.2 all-gather.13.cloned.1.call-start
  43.0 0.5 all-gather.13.cloned.1.call-update
  43.5 222.9 %all-to-all-done = bf16[16,160,2048]{2,1,0:T(8,128)(2,1)} async-done(((bf16[16,160,2048]{2,1,0:T(8,128)(2,1)}), bf16[16,160,2048]{2,1,0:T(8,128)(2,1)}, u32[]{:S(2)}, u32[]{:S(2)}) %all-to-all-start) | async-done | bytes 10485792 | tf_op jit(solution)/shard_map/all_to_all | solution.py:24
  266.4 10.1 %fusion.26 = (bf16[1,8,160,2048]{3,2,0,1:T(8,128)(2,1)}, bf16[1,8,160,2048]{3,2,0,1:T(8,128)(2,1)}) fusion(bf16[2,8,160,2048]{3,2,0,1:T(8,128)(2,1)} %bitcast.6), kind=kLoop, calls=%fused_computation.46 | loop fusion | bytes 20971520 | tf_op jit(solution)/shard_map/slice | solution.py:27
  276.5 0.0 all-gather.9.cloned.1.call-done
  276.5 14.0 %fusion.5 = f32[1280,1536]{1,0:T(8,128)} fusion(bf16[1280,2048]{1,0:T(8,128)(2,1)} %bitcast.53, bf16[1,2048,1536]{2,1,0:T(8,128)(2,1)} %all-gather.9.cloned.1.call-done), kind=kOutput, calls=%fused_computation.11 | convolution fusion | flops 8053063680 | bytes 19398656 | tf_op jit(solution)/shard_map/dot_general | solution.py:28
  290.5 0.0 all-gather.11.cloned.1.call-done
  290.5 10.9 %convolution_convert_fusion.1 = bf16[1280,2048]{1,0:T(8,128)(2,1)} fusion(bf16[1,768,2048]{2,1,0:T(8,128)(2,1)} %all-gather.11.cloned.1.call-done, f32[1280,1536]{1,0:T(8,128)} %fusion.5), kind=kOutput, calls=%fused_computation.8 | convolution fusion | flops 4035051520 | bytes 16252928 | tf_op jit(solution)/shard_map/dot_general | solution.py:38
  301.4 4.7 all-to-all-start.1
  306.0 0.3 all-gather.15.cloned.1.call-start
  306.3 0.3 all-gather.15.cloned.1.call-update
  306.6 0.0 all-gather.13.cloned.1.call-done
  306.6 14.0 %fusion.3 = f32[1280,1536]{1,0:T(8,128)} fusion(bf16[1280,2048]{1,0:T(8,128)(2,1)} %bitcast.52, bf16[1,2048,1536]{2,1,0:T(8,128)(2,1)} %all-gather.13.cloned.1.call-done), kind=kOutput, calls=%fused_computation.9 | convolution fusion | flops 8053063680 | bytes 19398656 | tf_op jit(solution)/shard_map/dot_general | solution.py:28
  320.6 33.1 %all-gather.15.cloned.1.call-done = bf16[1,768,2048]{2,1,0:T(8,128)(2,1)} async-done(((bf16[1,768,512]{2,1,0:T(8,128)(2,1)}), bf16[1,768,2048]{2,1,0:T(8,128)(2,1)}) %all-gather.15.cloned.1.call-update) | async-done | bytes 3145744 | tf_op jit(solution)/shard_map/all_gather | solution.py:40
  353.7 10.8 %convolution_convert_fusion = bf16[1280,2048]{1,0:T(8,128)(2,1)} fusion(bf16[1,768,2048]{2,1,0:T(8,128)(2,1)} %all-gather.15.cloned.1.call-done, f32[1280,1536]{1,0:T(8,128)} %fusion.3), kind=kOutput, calls=%fused_computation.7 | convolution fusion | flops 4035051520 | bytes 16252928 | tf_op jit(solution)/shard_map/dot_general | solution.py:38
  364.5 58.0 %all-to-all-done.1 = bf16[8,160,2048]{2,1,0:T(8,128)(2,1)} async-done(((bf16[8,160,2048]{2,1,0:T(8,128)(2,1)}), bf16[8,160,2048]{2,1,0:T(8,128)(2,1)}, u32[]{:S(2)}, u32[]{:S(2)}) %all-to-all-start.1) | async-done | bytes 5242912 | tf_op jit(solution)/shard_map/all_to_all | solution.py:37
  422.5 0.0 copy-start.3
  422.5 4.8 all-to-all-start.2
  427.3 0.0 copy-done.3
  427.3 0.1 copy.10
  427.5 116.3 %all-to-all-done.2 = bf16[8,160,2048]{2,1,0:T(8,128)(2,1)} async-done(((bf16[8,160,2048]{2,1,0:T(8,128)(2,1)}), bf16[8,160,2048]{2,1,0:T(8,128)(2,1)}, u32[]{:S(2)}, u32[]{:S(2)}) %all-to-all-start.2) | async-done | bytes 5242912 | tf_op jit(solution)/shard_map/all_to_all | solution.py:37
  543.7 12.7 %pad_maximum_fusion = bf16[2560,2048]{1,0:T(8,128)(2,1)} fusion(bf16[1280,2048]{1,0:T(8,128)(2,1)} %bitcast.17, bf16[1280,2048]{1,0:T(8,128)(2,1)} %bitcast.11), kind=kLoop, calls=%fused_computation.4 | loop fusion | flops 20971520 | bytes 20971520 | tf_op jit(solution)/shard_map/concatenate | solution.py:49
  556.4 0.0 copy-start.1
  556.4 22.0 %gather_fusion = bf16[2048,2048]{1,0:T(8,128)(2,1)} fusion(bf16[2560,2048]{1,0:T(8,128)(2,1)} %pad_maximum_fusion, s32[2048]{0:T(1024)S(1)} %broadcast_clamp_fusion), kind=kCustom, calls=%fused_computation | custom fusion | bytes 16785408 | tf_op jit(solution)/shard_map/gather | solution.py:53
  578.4 12.2 %fusion = bf16[256,2048]{1,0:T(8,128)(2,1)} fusion(bf16[2048,2048]{1,0:T(8,128)(2,1)} %gather_fusion, f32[256,8]{1,0:T(8,128)S(1)} %copy.10), kind=kLoop, calls=%fused_computation.3 | loop fusion | flops 12058624 | bytes 9445376 | tf_op jit(solution)/shard_map/reduce_sum | solution.py:55
  590.6 0.0 copy-done.1
  (4 shorter events, 0.0 us)
Async XLA Ops:
  6.5 6.7 %copy-start = (bf16[256,2048]{1,0:T(8,128)(2,1)S(1)}, bf16[256,2048]{1,0:T(8,128)(2,1)}, u32[]{:S(2)}) copy-start(bf16[256,2048]{1,0:T(8,128)(2,1)} %param.5) | copy-start | bytes 3145732
  31.1 235.3 %all-to-all-start = ((bf16[16,160,2048]{2,1,0:T(8,128)(2,1)}), bf16[16,160,2048]{2,1,0:T(8,128)(2,1)}, u32[]{:S(2)}, u32[]{:S(2)}) async-start(bf16[16,160,2048]{2,1,0:T(8,128)(2,1)} %bitcast.51), calls=%async_computation | async-start | bytes 20971520 | tf_op jit(solution)/shard_map/all_to_all | solution.py:24
  37.5 4.0 copy-start.2
  37.5 239.0 %all-gather.9.cloned.1.call-start = ((), (), s32[]{:S(2)}) async-start(), calls=%async_computation.3 | async-start | bytes 7864320 | tf_op jit(solution)/shard_map/all_gather | solution.py:30
  41.4 249.1 %all-gather.11.cloned.1.call-start = ((), (), s32[]{:S(2)}) async-start(), calls=%async_computation.4 | async-start | bytes 3932160 | tf_op jit(solution)/shard_map/all_gather | solution.py:40
  42.8 263.8 %all-gather.13.cloned.1.call-start = ((), (), s32[]{:S(2)}) async-start(), calls=%async_computation.5 | async-start | bytes 7864320 | tf_op jit(solution)/shard_map/all_gather | solution.py:30
  301.4 121.1 %all-to-all-start.1 = ((bf16[8,160,2048]{2,1,0:T(8,128)(2,1)}), bf16[8,160,2048]{2,1,0:T(8,128)(2,1)}, u32[]{:S(2)}, u32[]{:S(2)}) async-start(bf16[8,160,2048]{2,1,0:T(8,128)(2,1)} %bitcast.54), calls=%async_computation.1 | async-start | bytes 10485760 | tf_op jit(solution)/shard_map/all_to_all | solution.py:37
  306.0 47.6 %all-gather.15.cloned.1.call-start = ((), (), s32[]{:S(2)}) async-start(), calls=%async_computation.6 | async-start | bytes 3932160 | tf_op jit(solution)/shard_map/all_gather | solution.py:40
  422.5 4.8 copy-start.3
  422.5 121.2 %all-to-all-start.2 = ((bf16[8,160,2048]{2,1,0:T(8,128)(2,1)}), bf16[8,160,2048]{2,1,0:T(8,128)(2,1)}, u32[]{:S(2)}, u32[]{:S(2)}) async-start(bf16[8,160,2048]{2,1,0:T(8,128)(2,1)} %bitcast.55), calls=%async_computation.2 | async-start | bytes 10485760 | tf_op jit(solution)/shard_map/all_to_all | solution.py:37
  556.4 34.2 %copy-start.1 = (bf16[256,2048]{1,0:T(8,128)(2,1)S(1)}, bf16[256,2048]{1,0:T(8,128)(2,1)}, u32[]{:S(2)}) copy-start(bf16[256,2048]{1,0:T(8,128)(2,1)} %param.5) | copy-start | bytes 3145732
Sparse Core Ops, SparseCore 0:
  41.5 71.6 all-gather.8
  115.0 43.6 all-gather.10
  160.6 70.0 all-gather.12
  308.4 45.2 all-gather.14
where the time goes:
time: 605 us; the launch traced here: 598 us
  waiting for transfers between devices  431 us (71%)
  local copies, waits for them, and re-layouts  56.9 us (9%)
  matrix products  49.6 us (8%)
  other arithmetic  29.9 us (5%)
  starting transfers between devices  16.3 us (3%)
  between operations  13.7 us (2%)
    all_to_all x1, waiting for transfers between devices, shards(): lax.all_to_all(send_buffer, 'expert', split_axis=0, concat_axis=1, tiled=...  223 us
    all_to_all x2, waiting for transfers between devices, shards(): lax.all_to_all(jnp.dot(hidden, lax.all_gather(w_down[local_expert], 'dp',...  174 us
    all_gather x2, waiting for transfers between devices, shards(): lax.all_gather(w_down[local_expert], 'dp', axis=1, tiled=True)  33.1 us
    dot_general x2, matrix products, shards(): jnp.dot(rows_in, lax.all_gather(w_gate_up[local_expert], 'dp', axis=0, ti...  27.9 us
    gather x1, local copies, waits for them, and re-layouts, shards(): gathered = returned[source_rows].reshape(tok_rows, top_count, model_width)  22 us
    dot_general x2, matrix products, shards(): jnp.dot(hidden, lax.all_gather(w_down[local_expert], 'dp', axis=1, tiled=...  21.7 us
    scatter x1, local copies, waits for them, and re-layouts, shards(): jnp.zeros((experts * capacity, model_width), jnp.bfloat16).at[target]  17.9 us
    concatenate x1, other arithmetic, shards(): returned = jnp.concatenate(returned_list, axis=0)  12.7 us
  transfers between devices with their start and end apart: 7, of which 4 were waited for; matrix products, arithmetic and copies ran while one was open for 11% of the time, Pallas kernels for 0%

commit v1 on v0

v1 whole, which is shorter than its diff:
```python
import functools

import jax
import jax.numpy as jnp
from jax import lax
from jax.experimental import pallas as pl
from jax.experimental.pallas import tpu as pltpu
from jax.sharding import PartitionSpec as P

MESH = pl.DeviceIdType.MESH


def xor(index, mask):
    width = 1
    while width <= mask:
        if mask & width:
            index = index + width * (1 - 2 * lax.rem(index // width, 2))
        width *= 2
    return index


def span(masks):
    out = [0]
    for m in masks:
        out = out + [m ^ s for s in out]
    return out


class Gather:
    def __init__(self, orders, me, target, own, slot, send_sem, recv_sem):
        self.orders, self.me, self.target = orders, me, target
        self.own, self.slot = own, slot
        self.send_sem, self.recv_sem = send_sem, recv_sem
        self.started = []

    def stages(self):
        return len(self.orders[0])

    def send(self, stage):
        for half, order in enumerate(self.orders):
            g = order[stage]
            for s in span(order[:stage]):
                block = xor(self.me, s)
                dst = self.slot(block, half)
                copy = pltpu.make_async_remote_copy(
                    src_ref=self.own(half) if s == 0 else dst,
                    dst_ref=dst,
                    send_sem=self.send_sem.at[half, g ^ s],
                    recv_sem=self.recv_sem.at[half, g ^ s],
                    device_id=self.target(xor(self.me, g)),
                    device_id_type=MESH,
                )
                copy.start()
                self.started.append(copy)

    def wait(self, stage):
        for half, order in enumerate(self.orders):
            g = order[stage]
            for s in span(order[:stage]):
                ref = self.slot(xor(self.me, g ^ s), half)
                pltpu.make_async_remote_copy(
                    src_ref=ref,
                    dst_ref=ref,
                    send_sem=self.send_sem.at[half, g ^ s],
                    recv_sem=self.recv_sem.at[half, g ^ s],
                    device_id=self.target(xor(self.me, g)),
                    device_id_type=MESH,
                ).wait_recv()

    def drain(self):
        for copy in self.started:
            copy.wait_send()


def powers(count):
    out, width = [], 1
    while width < count:
        out.append(width)
        width *= 2
    return out


def kernel(
    dps, owners,
    tok_in, share_in, gu_in, dn_in, got,
    tok, share, gu, dn, hid, sib,
    tok_s, tok_r, share_s, share_r, gu_s, gu_r, dn_s, dn_r, sib_s, sib_r, out_s, out_r, loc,
):
    dp, ex = lax.axis_index("dp"), lax.axis_index("expert")
    chips = owners // 2
    chip, core = ex // 2, lax.rem(ex, 2)
    local = gu_in.shape[0]
    depth = gu_in.shape[1]
    cols = dn_in.shape[2]
    rows, width = tok_in.shape
    ff = dn_in.shape[1]

    dp_masks = powers(dps)
    chip_masks = [2 * (2 * w - 1) for w in powers(chips)]

    barrier = pltpu.get_barrier_semaphore()
    peers = [(xor(dp, m), ex) for m in dp_masks] + [(dp, xor(ex, r)) for r in range(1, owners)]
    for peer in peers:
        pl.semaphore_signal(barrier, inc=1, device_id=peer, device_id_type=MESH)
    pl.semaphore_wait(barrier, len(peers))

    def on_expert(index):
        return (dp, index)

    def on_dp(index):
        return (index, ex)

    half_rows, half_depth, half_ff = rows // 2, depth // 2, ff // 2
    tokens = Gather(
        [chip_masks + [1], chip_masks[::-1] + [1]], ex, on_expert,
        lambda h: tok_in.at[pl.ds(h * half_rows, half_rows)],
        lambda b, h: tok.at[b // 2, lax.rem(b, 2), pl.ds(h * half_rows, half_rows)],
        tok_s, tok_r,
    )
    ups = [
        Gather(
            [dp_masks, dp_masks[::-1]], dp, on_dp,
            lambda h, e=e: gu_in.at[e, pl.ds(h * half_depth, half_depth)],
            lambda b, h, e=e: gu.at[e, pl.ds(pl.multiple_of(b * depth + h * half_depth, half_depth), half_depth)],
            gu_s.at[e], gu_r.at[e],
        )
        for e in range(local)
    ]
    down = Gather(
        [dp_masks, dp_masks[::-1]], dp, on_dp,
        lambda h: dn_in.at[:, pl.ds(h * half_ff, half_ff)],
        lambda b, h: dn.at[b, :, pl.ds(h * half_ff, half_ff)],
        dn_s, dn_r,
    )

    tokens.send(0)
    for e in range(local):
        ups[e].send(0)
    shares = []
    for r in range(1, owners):
        copy = pltpu.make_async_remote_copy(
            src_ref=share_in.at[xor(ex, r)], dst_ref=share.at[ex],
            send_sem=share_s.at[r], recv_sem=share_r.at[r],
            device_id=(dp, xor(ex, r)), device_id_type=MESH,
        )
        copy.start()
        shares.append(copy)
    locals_ = [
        pltpu.make_async_copy(tok_in, tok.at[chip, core], loc.at[0]),
        pltpu.make_async_copy(share_in.at[ex], share.at[ex], loc.at[1]),
        pltpu.make_async_copy(
            gu_in, gu.at[:, pl.ds(pl.multiple_of(dp * depth, depth), depth)], loc.at[2]
        ),
        pltpu.make_async_copy(dn_in, dn.at[dp], loc.at[3]),
    ]
    for copy in locals_:
        copy.start()

    last = len(dp_masks) - 1
    queue = [(g, stage) for g in ups for stage in range(1, last + 1)]
    tok_stage, tok_last = 0, tokens.stages() - 1

    def step_tokens():
        nonlocal tok_stage
        if tok_stage < tok_last:
            tokens.wait(tok_stage)
            tok_stage += 1
            tokens.send(tok_stage)

    for at, (g, stage) in enumerate(queue):
        step_tokens()
        g.wait(stage - 1)
        g.send(stage)
        if at == 0:
            down.send(0)
    while tok_stage < tok_last:
        step_tokens()
    tokens.wait(tok_last)
    for copy in locals_:
        copy.wait()

    tile = 256 if ff % 256 == 0 else ff

    def hidden(e):
        def body(c, carry):
            x = tok[c].reshape(2 * rows, width)
            for f in range(ff // tile):
                a = jnp.dot(x, gu[e, :, f * tile:(f + 1) * tile], preferred_element_type=jnp.float32)
                b = jnp.dot(
                    x, gu[e, :, ff + f * tile:ff + (f + 1) * tile], preferred_element_type=jnp.float32
                )
                hid[e, c, :, f * tile:(f + 1) * tile] = (a / (1.0 + jnp.exp(-a)) * b).astype(hid.dtype)
            return carry

        lax.fori_loop(0, chips, body, 0)

    for e in range(local):
        ups[e].wait(last)
        hidden(e)
        if e == 0:
            for stage in range(1, last + 1):
                down.wait(stage - 1)
                down.send(stage)

    tokens.drain()
    for r, copy in enumerate(shares):
        pltpu.make_async_remote_copy(
            src_ref=share_in.at[0], dst_ref=share.at[xor(ex, r + 1)],
            send_sem=share_s.at[r + 1], recv_sem=share_r.at[r + 1],
            device_id=(dp, xor(ex, r + 1)), device_id_type=MESH,
        ).wait_recv()

    def partial(b):
        at = pl.ds(pl.multiple_of(b * cols, cols), cols)

        def body(c, carry):
            parts = [
                jnp.dot(hid[e, c], dn[b, e], preferred_element_type=jnp.float32) for e in range(local)
            ]
            for k in range(2):
                scale = jnp.transpose(share[2 * c + k])
                total = parts[0][k * rows:(k + 1) * rows] * scale[:, 0:1]
                for e in range(1, local):
                    total = total + parts[e][k * rows:(k + 1) * rows] * scale[:, e:e + 1]
                tok[c, k, :, at] = total.astype(tok.dtype)
            return carry

        lax.fori_loop(0, chips, body, 0)

    def to_sibling(s, b):
        at = pl.ds(pl.multiple_of(b * cols, cols), cols)
        copy = pltpu.make_async_remote_copy(
            src_ref=tok.at[:, 1 - core, :, at], dst_ref=sib.at[:, :, at],
            send_sem=sib_s.at[s], recv_sem=sib_r.at[s],
            device_id=(dp, xor(ex, 1)), device_id_type=MESH,
        )
        return copy

    sent = []

    def combine(s, b):
        at = pl.ds(pl.multiple_of(b * cols, cols), cols)

        def body(c, carry):
            tok[c, core, :, at] = (
                tok[c, core, :, at].astype(jnp.float32) + sib[c, :, at].astype(jnp.float32)
            ).astype(tok.dtype)
            return carry

        lax.fori_loop(0, chips, body, 0)
        for r in range(1, chips):
            other = xor(chip, r)
            copy = pltpu.make_async_remote_copy(
                src_ref=tok.at[other, core, :, at], dst_ref=got.at[chip, :, at],
                send_sem=out_s.at[s, r], recv_sem=out_r.at[s, r],
                device_id=(dp, xor(ex, 2 * r)), device_id_type=MESH,
            )
            copy.start()
            sent.append(copy)
        own = pltpu.make_async_copy(tok.at[chip, core, :, at], got.at[chip, :, at], out_r.at[s, 0])
        own.start()
        sent.append(own)

    pending = None
    for s in range(dps):
        b = xor(dp, s)
        if s == 1:
            down.wait(last)
        partial(b)
        copy = to_sibling(s, b)
        copy.start()
        if pending is not None:
            pending[2].wait()
            combine(pending[0], pending[1])
        pending = (s, b, copy)
    pending[2].wait()
    combine(pending[0], pending[1])

    for s in range(dps):
        b = xor(dp, s)
        at = pl.ds(pl.multiple_of(b * cols, cols), cols)
        for r in range(1, chips):
            pltpu.make_async_remote_copy(
                src_ref=tok.at[chip, core, :, at], dst_ref=got.at[xor(chip, r), :, at],
                send_sem=out_s.at[s, r], recv_sem=out_r.at[s, r],
                device_id=(dp, xor(ex, 2 * r)), device_id_type=MESH,
            ).wait_recv()
    for at, copy in enumerate(sent):
        if at % chips == chips - 1:
            copy.wait()
        else:
            copy.wait_send()
    for copy in shares:
        copy.wait_send()
    for g in ups + [down]:
        g.drain()


def shards(tokens, expert_ids, route_probs, w_gate_up, w_down):
    dps, owners = lax.axis_size("dp"), lax.axis_size("expert")
    chips = owners // 2
    local, depth, both = w_gate_up.shape
    experts = owners * local
    rows, width = tokens.shape
    ff, cols = w_down.shape[1:]
    weights = route_probs / jnp.sum(route_probs, axis=1, keepdims=True)
    share = jnp.sum(
        jnp.where(
            expert_ids.T[None] == jnp.arange(experts, dtype=jnp.int32)[:, None, None],
            weights.T[None], 0.0,
        ),
        axis=1,
    ).reshape(owners, local, rows)
    pad = -local % 8
    share = jnp.pad(share, ((0, 0), (0, pad), (0, 0)))
    any_ = pl.BlockSpec(memory_space=pl.ANY)
    dma = pltpu.SemaphoreType.DMA
    bf16 = jnp.bfloat16
    got = pl.pallas_call(
        functools.partial(kernel, dps, owners),
        out_shape=jax.ShapeDtypeStruct((chips, rows, width), bf16),
        in_specs=[any_] * 4,
        out_specs=any_,
        scratch_shapes=[
            pltpu.VMEM((chips, 2, rows, width), bf16),
            pltpu.VMEM((owners, local + pad, rows), jnp.float32),
            pltpu.VMEM((local, dps * depth, both), bf16),
            pltpu.VMEM((dps, local, ff, cols), bf16),
            pltpu.VMEM((local, chips, 2 * rows, ff), bf16),
            pltpu.VMEM((chips, rows, width), bf16),
            dma((2, owners)), dma((2, owners)),
            dma((owners,)), dma((owners,)),
            dma((local, 2, dps)), dma((local, 2, dps)),
            dma((2, dps)), dma((2, dps)),
            dma((dps,)), dma((dps,)),
            dma((dps, chips)), dma((dps, chips)),
            dma((4,)),
        ],
        compiler_params=pltpu.CompilerParams(
            collective_id=0, has_side_effects=True, vmem_limit_bytes=67043328
        ),
    )(tokens, share, w_gate_up, w_down)
    return jnp.sum(got.astype(jnp.float32), axis=0).astype(bf16)


def solution(mesh):
    return jax.shard_map(
        shards,
        mesh=mesh,
        in_specs=(
            P(("dp", "expert"), None),
            P(("dp", "expert"), None),
            P(("dp", "expert"), None),
            P("expert", "dp", None),
            P("expert", None, "dp"),
        ),
        out_specs=P(("dp", "expert"), None),
        check_vma=False,
    )
```

time: 605 us -> 261 us (0.43)
  waiting for transfers between devices: 431 us -> 0 us
  Pallas kernels: 0 us -> 252 us
  local copies, waits for them, and re-layouts: 56.9 us -> 0.65 us
  matrix products: 49.6 us -> 0 us
  other arithmetic: 29.9 us -> 6.41 us
  starting transfers between devices: 16.3 us -> 0 us
  between operations: 13.7 us -> 0.02 us
    all_to_all x3 -> x0, waiting for transfers between devices: 397 us -> none  [the longest x1 223 us: shards(): lax.all_to_all(send_buffer, 'expert', split_axis=0, concat_axis=1, tiled=...]
    pallas_call x0 -> x1, Pallas kernels: none -> 252 us  [shards(): pl.pallas_call(functools.partial(kernel, dps, owners), out_shape=jax.Shap...]
    dot_general x4 -> x0, matrix products: 49.6 us -> none  [the longest x2 27.9 us: shards(): jnp.dot(rows_in, lax.all_gather(w_gate_up[local_expert], 'dp', axis=0, ti...]
    all_gather x4 -> x0, waiting for transfers between devices: 33.1 us -> none  [the longest x2 33.1 us: shards(): lax.all_gather(w_down[local_expert], 'dp', axis=1, tiled=True)]
    gather x1 -> x0, local copies, waits for them, and re-layouts: 22 us -> none  [shards(): gathered = returned[source_rows].reshape(tok_rows, top_count, model_width)]
    scatter x1 -> x0, local copies, waits for them, and re-layouts: 17.9 us -> none  [shards(): jnp.zeros((experts * capacity, model_width), jnp.bfloat16).at[target]]
    all_to_all x3 -> x0, starting transfers between devices: 15.8 us -> none  [the longest x2 9.44 us: shards(): lax.all_to_all(jnp.dot(hidden, lax.all_gather(w_down[local_expert], 'dp',...]
    slice x4 -> x0, local copies, waits for them, and re-layouts: 15.6 us -> none  [the longest x1 10.1 us: shards(): rows_in = received[local_expert]]
  transfers between devices with their start and end apart: 7 -> 0, of which waited for: 4 -> 0; matrix products, arithmetic and copies ran while one was open for 11% -> 0% of each run, Pallas kernels for 0% -> 0%
where the time goes in v1:
time: 261 us; the launch traced here: 259 us
  Pallas kernels  252 us (97%)
  other arithmetic  6.41 us (2%)
    pallas_call x1, Pallas kernels, shards(): pl.pallas_call(functools.partial(kernel, dps, owners), out_shape=jax.Shap...  252 us

profile of v1, /device:TPU:0, one launch (start us, length us, event | category | flops | bytes accessed | tf_op | source)
XLA Modules:
  0.0 258.8 jit_solution(10852010874391059281)
XLA Ops:
  0.0 0.7 reduce_sum.30
  0.7 0.7 divide_bitcast_fusion
  1.4 0.7 select_reduce_fusion
  2.2 0.6 pad.4.share_in
  2.8 251.7 %shard_map.55 = bf16[4,256,2048]{2,1,0:T(8,128)(2,1)} custom-call(bf16[256,2048]{1,0:T(8,128)(2,1)} %tok_in.1, f32[8,8,256]{2,1,0:T(8,128)} %pad.4.share_in, bf16[2,512,1536]{2,1,0:T(8,128)(2,1)} %gu_in.1, bf16[2,768,512]{2,1,0:T(8,128)(2,1)} %dn_in.1), custom_call_target="tpu_custom_call" | custom-call | tf_op jit(solution)/shard_map/pallas_call | solution.py:319
  254.6 4.3 %reduce_sum.32 = bf16[256,2048]{1,0:T(8,128)(2,1)} reduce(bf16[4,256,2048]{2,1,0:T(8,128)(2,1)} %shard_map.55, bf16[]{:T(256)} %constant.5.clone.1), dimensions={0}, to_apply=%region_2.3 | reduce | flops 1572864 | bytes 5242882 | tf_op jit(solution)/shard_map/reduce_sum | solution.py:343
  (1 shorter events, 0.0 us)

commit v2 on v1

--- a/solution.py
+++ b/solution.py
@@ -83,12 +83,13 @@
 def kernel(
     dps, owners,
     tok_in, share_in, gu_in, dn_in, got,
-    tok, share, gu, dn, hid, sib,
-    tok_s, tok_r, share_s, share_r, gu_s, gu_r, dn_s, dn_r, sib_s, sib_r, out_s, out_r, loc,
+    tok, share, gu, dn, hid, sib, near,
+    tok_s, tok_r, share_s, share_r, gu_s, gu_r, dn_s, dn_r, sib_s, sib_r, near_s, near_r, out_s, out_r, loc,
 ):
     dp, ex = lax.axis_index("dp"), lax.axis_index("expert")
-    chips = owners // 2
+    chips, pairs = owners // 2, owners // 4
     chip, core = ex // 2, lax.rem(ex, 2)
+    pair, side = chip // 2, lax.rem(chip, 2)
     local = gu_in.shape[0]
     depth = gu_in.shape[1]
     cols = dn_in.shape[2]
@@ -114,7 +115,7 @@
     tokens = Gather(
         [chip_masks + [1], chip_masks[::-1] + [1]], ex, on_expert,
         lambda h: tok_in.at[pl.ds(h * half_rows, half_rows)],
-        lambda b, h: tok.at[b // 2, lax.rem(b, 2), pl.ds(h * half_rows, half_rows)],
+        lambda b, h: tok.at[b // 4, lax.rem(b // 2, 2), lax.rem(b, 2), pl.ds(h * half_rows, half_rows)],
         tok_s, tok_r,
     )
     ups = [
@@ -146,7 +147,7 @@
         copy.start()
         shares.append(copy)
     locals_ = [
-        pltpu.make_async_copy(tok_in, tok.at[chip, core], loc.at[0]),
+        pltpu.make_async_copy(tok_in, tok.at[pair, side, core], loc.at[0]),
         pltpu.make_async_copy(share_in.at[ex], share.at[ex], loc.at[1]),
         pltpu.make_async_copy(
             gu_in, gu.at[:, pl.ds(pl.multiple_of(dp * depth, depth), depth)], loc.at[2]
@@ -171,8 +172,7 @@
         step_tokens()
         g.wait(stage - 1)
         g.send(stage)
-        if at == 0:
-            down.send(0)
+    down.send(0)
     while tok_stage < tok_last:
         step_tokens()
     tokens.wait(tok_last)
@@ -183,7 +183,7 @@
 
     def hidden(e):
         def body(c, carry):
-            x = tok[c].reshape(2 * rows, width)
+            x = tok[c // 2, lax.rem(c, 2)].reshape(2 * rows, width)
             for f in range(ff // tile):
                 a = jnp.dot(x, gu[e, :, f * tile:(f + 1) * tile], preferred_element_type=jnp.float32)
                 b = jnp.dot(
@@ -222,7 +222,7 @@
                 total = parts[0][k * rows:(k + 1) * rows] * scale[:, 0:1]
                 for e in range(1, local):
                     total = total + parts[e][k * rows:(k + 1) * rows] * scale[:, e:e + 1]
-                tok[c, k, :, at] = total.astype(tok.dtype)
+                tok[c // 2, lax.rem(c, 2), k, :, at] = total.astype(tok.dtype)
             return carry
 
         lax.fori_loop(0, chips, body, 0)
@@ -230,63 +230,86 @@
     def to_sibling(s, b):
         at = pl.ds(pl.multiple_of(b * cols, cols), cols)
         copy = pltpu.make_async_remote_copy(
-            src_ref=tok.at[:, 1 - core, :, at], dst_ref=sib.at[:, :, at],
+            src_ref=tok.at[:, :, 1 - core, :, at], dst_ref=sib.at[:, :, :, at],
             send_sem=sib_s.at[s], recv_sem=sib_r.at[s],
             device_id=(dp, xor(ex, 1)), device_id_type=MESH,
         )
         return copy
 
+    def add(c, side_, ref, at):
+        tok[c, side_, core, :, at] = (
+            tok[c, side_, core, :, at].astype(jnp.float32) + ref[...].astype(jnp.float32)
+        ).astype(tok.dtype)
+
+    def to_near(s, b):
+        at = pl.ds(pl.multiple_of(b * cols, cols), cols)
+
+        def body(c, carry):
+            add(c, 1 - side, sib.at[c, 1 - side, :, at], at)
+            return carry
+
+        lax.fori_loop(0, pairs, body, 0)
+
+        def body_own(c, carry):
+            add(c, side, sib.at[c, side, :, at], at)
+            return carry
+
+        lax.fori_loop(0, pairs, body_own, 0)
+        return pltpu.make_async_remote_copy(
+            src_ref=tok.at[:, 1 - side, core, :, at], dst_ref=near.at[:, :, at],
+            send_sem=near_s.at[s], recv_sem=near_r.at[s],
+            device_id=(dp, xor(ex, 2)), device_id_type=MESH,
+        )
+
     sent = []
 
-    def combine(s, b):
+    def home(s, b):
         at = pl.ds(pl.multiple_of(b * cols, cols), cols)
 
         def body(c, carry):
-            tok[c, core, :, at] = (
-                tok[c, core, :, at].astype(jnp.float32) + sib[c, :, at].astype(jnp.float32)
-            ).astype(tok.dtype)
-            return carry
-
-        lax.fori_loop(0, chips, body, 0)
-        for r in range(1, chips):
-            other = xor(chip, r)
+            add(c, side, near.at[c, :, at], at)
+            return carry
+
+        lax.fori_loop(0, pairs, body, 0)
+        for r in range(1, pairs):
             copy = pltpu.make_async_remote_copy(
-                src_ref=tok.at[other, core, :, at], dst_ref=got.at[chip, :, at],
+                src_ref=tok.at[xor(pair, r), side, core, :, at], dst_ref=got.at[pair, :, at],
                 send_sem=out_s.at[s, r], recv_sem=out_r.at[s, r],
-                device_id=(dp, xor(ex, 2 * r)), device_id_type=MESH,
+                device_id=(dp, xor(ex, 4 * r)), device_id_type=MESH,
             )
             copy.start()
             sent.append(copy)
-        own = pltpu.make_async_copy(tok.at[chip, core, :, at], got.at[chip, :, at], out_r.at[s, 0])
+        own = pltpu.make_async_copy(tok.at[pair, side, core, :, at], got.at[pair, :, at], out_r.at[s, 0])
         own.start()
         sent.append(own)
 
-    pending = None
+    first, second = {}, {}
+    for s in range(dps + 2):
+        if s < dps:
+            if s == 1:
+                down.wait(last)
+            partial(xor(dp, s))
+            first[s] = to_sibling(s, xor(dp, s))
+            first[s].start()
+        if 1 <= s < dps + 1:
+            first[s - 1].wait()
+            second[s - 1] = to_near(s - 1, xor(dp, s - 1))
+            second[s - 1].start()
+        if s >= 2:
+            second[s - 2].wait()
+            home(s - 2, xor(dp, s - 2))
+
     for s in range(dps):
         b = xor(dp, s)
-        if s == 1:
-            down.wait(last)
-        partial(b)
-        copy = to_sibling(s, b)
-        copy.start()
-        if pending is not None:
-            pending[2].wait()
-            combine(pending[0], pending[1])
-        pending = (s, b, copy)
-    pending[2].wait()
-    combine(pending[0], pending[1])
-
-    for s in range(dps):
-        b = xor(dp, s)
-        at = pl.ds(pl.multiple_of(b * cols, cols), cols)
-        for r in range(1, chips):
+        at = pl.ds(pl.multiple_of(b * cols, cols), cols)
+        for r in range(1, pairs):
             pltpu.make_async_remote_copy(
-                src_ref=tok.at[chip, core, :, at], dst_ref=got.at[xor(chip, r), :, at],
+                src_ref=tok.at[pair, side, core, :, at], dst_ref=got.at[xor(pair, r), :, at],
                 send_sem=out_s.at[s, r], recv_sem=out_r.at[s, r],
-                device_id=(dp, xor(ex, 2 * r)), device_id_type=MESH,
+                device_id=(dp, xor(ex, 4 * r)), device_id_type=MESH,
             ).wait_recv()
     for at, copy in enumerate(sent):
-        if at % chips == chips - 1:
+        if at % pairs == pairs - 1:
             copy.wait()
         else:
             copy.wait_send()
@@ -298,7 +321,7 @@
 
 def shards(tokens, expert_ids, route_probs, w_gate_up, w_down):
     dps, owners = lax.axis_size("dp"), lax.axis_size("expert")
-    chips = owners // 2
+    chips, pairs = owners // 2, owners // 4
     local, depth, both = w_gate_up.shape
     experts = owners * local
     rows, width = tokens.shape
@@ -318,22 +341,24 @@
     bf16 = jnp.bfloat16
     got = pl.pallas_call(
         functools.partial(kernel, dps, owners),
-        out_shape=jax.ShapeDtypeStruct((chips, rows, width), bf16),
+        out_shape=jax.ShapeDtypeStruct((pairs, rows, width), bf16),
         in_specs=[any_] * 4,
         out_specs=any_,
         scratch_shapes=[
-            pltpu.VMEM((chips, 2, rows, width), bf16),
+            pltpu.VMEM((pairs, 2, 2, rows, width), bf16),
             pltpu.VMEM((owners, local + pad, rows), jnp.float32),
             pltpu.VMEM((local, dps * depth, both), bf16),
             pltpu.VMEM((dps, local, ff, cols), bf16),
             pltpu.VMEM((local, chips, 2 * rows, ff), bf16),
-            pltpu.VMEM((chips, rows, width), bf16),
+            pltpu.VMEM((pairs, 2, rows, width), bf16),
+            pltpu.VMEM((pairs, rows, width), bf16),
             dma((2, owners)), dma((2, owners)),
             dma((owners,)), dma((owners,)),
             dma((local, 2, dps)), dma((local, 2, dps)),
             dma((2, dps)), dma((2, dps)),
             dma((dps,)), dma((dps,)),
-            dma((dps, chips)), dma((dps, chips)),
+            dma((dps,)), dma((dps,)),
+            dma((dps, pairs)), dma((dps, pairs)),
             dma((4,)),
         ],
         compiler_params=pltpu.CompilerParams(

time: 261 us -> 250 us (0.958)
  Pallas kernels: 252 us -> 244 us
    pallas_call x1, Pallas kernels: 252 us -> 244 us  [shards(): pl.pallas_call(functools.partial(kernel, dps, owners), out_shape=jax.Shap...]
where the time goes in v2:
time: 250 us
  Pallas kernels  244 us (98%)
  other arithmetic  5.47 us (2%)
    pallas_call x1, Pallas kernels, shards(): pl.pallas_call(functools.partial(kernel, dps, owners), out_shape=jax.Shap...  244 us

profile of v2, /device:TPU:0, one launch (start us, length us, event | category | flops | bytes accessed | tf_op | source)
XLA Modules:
  0.0 249.6 jit_solution(6223632030234905862)
XLA Ops:
  0.0 0.7 reduce_sum.30
  0.7 0.7 divide_bitcast_fusion
  1.4 0.7 select_reduce_fusion
  2.2 0.6 pad.4.share_in
  2.8 243.5 %shard_map.55 = bf16[2,256,2048]{2,1,0:T(8,128)(2,1)} custom-call(bf16[256,2048]{1,0:T(8,128)(2,1)} %tok_in.1, f32[8,8,256]{2,1,0:T(8,128)} %pad.4.share_in, bf16[2,512,1536]{2,1,0:T(8,128)(2,1)} %gu_in.1, bf16[2,768,512]{2,1,0:T(8,128)(2,1)} %dn_in.1), custom_call_target="tpu_custom_call" | custom-call | tf_op jit(solution)/shard_map/pallas_call | solution.py:342
  246.3 3.3 %reduce_sum.32 = bf16[256,2048]{1,0:T(8,128)(2,1)} reduce(bf16[2,256,2048]{2,1,0:T(8,128)(2,1)} %shard_map.55, bf16[]{:T(256)} %constant.5.clone.1), dimensions={0}, to_apply=%region_2.3 | reduce | flops 524288 | bytes 3145730 | tf_op jit(solution)/shard_map/reduce_sum | solution.py:368
  (1 shorter events, 0.0 us)
